TPU v7x, 512 devices: a whole 4x4x16 slice. The times are simulated.
512 devices in a mesh: doc: 8 (over x, core), seq: 64 (over z, y).
Axes of the slice: x: 4, y: 4, z: 16, core: 2. Of those that a mesh axis runs over, the one named last changes fastest.
Arguments:
- queries: bfloat16 [65536, 1792], P(('doc', 'seq')), parts along dimension 0, may hold values from -5 to 5
- keys: bfloat16 [65536, 256], P(('doc', 'seq')), parts along dimension 0, may hold values from -5 to 5
- values: bfloat16 [65536, 256], P(('doc', 'seq')), parts along dimension 0, may hold values from -6 to 6
- doc_length: int32 [8], P('doc'), parts along dimension 0, may hold values from 4096 to 8192
- sink_pos: int32 [32], P('doc'), parts along dimension 0, may hold values from 0 to 127, as said below
Outputs:
- attended: bfloat16 [65536, 1792], P(('doc', 'seq')), parts along dimension 0
- row_lse: float32 [14, 65536], P(None, ('doc', 'seq')), parts along dimension 1
- sink_mass: float32 [14, 65536], P(None, ('doc', 'seq')), parts along dimension 1
- head_lse: float32 [112], P('doc'), parts along dimension 0
- head_sink: float32 [112], P('doc'), parts along dimension 0
There are 8 independent parts, one for each index of `doc`. A program takes and returns all parts, laid end to end along the dimension named above; each array names one. Nothing has to cross between parts.
Inputs may be any that keep to these rules, and one draw needn't show every extreme that they name: `sink_pos`: 4 distinct positions within the document's first 128 tokens; positions 0 and 127 are always among them. Positions from doc_length up to 8192 are padding.
All inputs are finite; a program needn't handle non-finite values.
Results may differ from a plain program's by a relative error of at most 0.009.
Values may be sent and summed in bfloat16 or wider, within the bound.
A program may use at most 64 MiB of HBM per device.

v0:
```python
import functools

import jax
import jax.numpy as jnp
from jax import lax
from jax.experimental import pallas as pl
from jax.experimental.pallas import tpu as pltpu
from jax.sharding import PartitionSpec as P

D = 128
ROWS = 128
GROUP = 7
HALF = GROUP * D
FLAT = GROUP * ROWS
YS = 4
LOG2E = 1.4426950408889634
LN2 = 0.6931471805599453
SCALE = LOG2E * D**-0.5
NEG = -1e30
MESH = pl.DeviceIdType.MESH
TILES = ((0, 2), (2, 4), (4, 7))
OWN, PART, HEAD, DIAG = range(4)
Q_HEAD_0, Q_PART, Q_HEAD_1, Q_DIAG = 2, 3, 4, 8


def kernel(
    zs, q_ref, k_ref, v_ref, len_ref, sink_ref,
    att_ref, lse_ref, mass_ref, tot_ref,
    kv, xbuf, qbuf, qsend, acc, l_acc, m_acc, obuf, rx, fin, fin_rx, statb, stats, red, wts,
    ring_send, ring_recv, x_send, x_recv, q_send, q_recv, st_send, st_recv, o_send, o_recv,
    red_send, red_recv,
):
    fs = zs // 2
    seq = lax.axis_index("seq")
    z, y = seq // YS, seq % YS
    head = ((y + 1) // 2) % 2
    part = y // 2
    y_head = y + 1 - 2 * (y % 2)
    y_part = 3 - y
    y_diag = y_part + 1 - 2 * (y_part % 2)
    right, left = (z + 1) % zs, (z + zs - 1) % zs
    base = z * YS

    def at(zz, yy):
        return {"seq": zz * YS + yy}

    def remote(src, dst, send, recv, target):
        return pltpu.make_async_remote_copy(
            src_ref=src, dst_ref=dst, send_sem=send, recv_sem=recv, device_id=target, device_id_type=MESH
        )

    first = head == 0
    mine = y % 2
    for i, ref in enumerate((k_ref, v_ref)):
        lo, hi = ref[:, :D], ref[:, D:]
        kv[z, mine, i] = jnp.where(first, lo, hi)
        xbuf[i] = jnp.where(first, hi, lo)
    qlo, qhi = q_ref[:, :HALF], q_ref[:, HALF:]
    qbuf[OWN] = jnp.where(first, qlo, qhi)
    qsend[...] = jnp.where(first, qhi, qlo)

    barrier = pltpu.get_barrier_semaphore()
    for target in (at(right, y), at(left, y), at(z, y_head), at(z, y_part), at(z, y_diag)):
        pl.semaphore_signal(barrier, inc=1, device_id=target, device_id_type=MESH)
    pl.semaphore_wait(barrier, 5)

    def hop(direction, s, c, plane):
        return remote(
            kv.at[plane, c], kv.at[plane, c],
            ring_send.at[direction, s, c], ring_recv.at[direction, s + 1, c],
            at(right if direction == 0 else left, y),
        )

    def arrived(direction, s, c, plane):
        return remote(
            kv.at[plane, c], kv.at[plane, c],
            ring_send.at[direction, s - 1, c], ring_recv.at[direction, s, c],
            at(right if direction == 0 else left, y),
        )

    def q_copy(k):
        lo, hi = slice(0, 4 * D), slice(4 * D, HALF)
        src, dst, target = (
            (qsend.at[:, lo], qbuf.at[HEAD, :, lo], y_head),
            (qsend.at[:, hi], qbuf.at[HEAD, :, hi], y_head),
            (qbuf.at[OWN], qbuf.at[PART], y_part),
            (qbuf.at[HEAD, :, lo], qbuf.at[DIAG, :, lo], y_part),
            (qbuf.at[HEAD, :, hi], qbuf.at[DIAG, :, hi], y_part),
        )[k]
        return remote(src, dst, q_send.at[k], q_recv.at[k], at(z, target))

    other = 1 - mine
    to_head = remote(xbuf, kv.at[z, mine], x_send, x_recv, at(z, y_head))
    from_head = remote(xbuf, kv.at[z, other], x_send, x_recv, at(z, y_head))
    to_head.start()
    hop(0, 0, mine, z).start()
    hop(1, 0, mine, z).start()
    q_copy(0).start()
    q_copy(1).start()
    q_copy(2).start()
    from_head.wait_recv()
    hop(0, 0, other, z).start()
    hop(1, 0, other, z).start()

    def owner(b):
        return jnp.where(b == OWN, y, jnp.where(b == PART, y_part, jnp.where(b == HEAD, y_head, y_diag)))

    def scores(b, heads, key_mat):
        lo, hi = heads
        rows = jnp.concatenate([qbuf[b, :, j * D : (j + 1) * D] for j in range(lo, hi)], axis=0)
        s = lax.dot_general(rows, key_mat, (((1,), (1,)), ((), ())), preferred_element_type=jnp.float32)
        return [s[:, j : j + D] * SCALE for j in range(0, key_mat.shape[0], D)]

    def top(groups):
        best = groups[0]
        for g in groups[1:]:
            best = jnp.maximum(best, g)
        return jnp.broadcast_to(jnp.max(best, axis=1, keepdims=True), best.shape)

    def total(groups):
        out = groups[0]
        for g in groups[1:]:
            out = out + g
        return out

    def first_unit(b):
        key_mat = jnp.concatenate([kv[z, 0, 0], kv[z, 1, 0]], axis=0)
        val_mat = jnp.concatenate([kv[z, 0, 1], kv[z, 1, 1]], axis=0)
        for heads in TILES:
            n = (heads[1] - heads[0]) * ROWS
            rows = pl.ds(heads[0] * ROWS, n)
            gs = scores(b, heads, key_mat)
            row = lax.broadcasted_iota(jnp.int32, (n, D), 0) % ROWS + owner(b) * ROWS
            lane = lax.broadcasted_iota(jnp.int32, (n, D), 1) + part * (2 * ROWS)
            ok = [lane + j * D <= row for j in range(2)]
            gs = [jnp.where(o, g, 2 * NEG) for o, g in zip(ok, gs)]
            m = jnp.maximum(top(gs), NEG)
            ps = [jnp.exp2(g - m) for g in gs]
            m_acc[b, rows] = m
            l_acc[b, rows] = total(ps)
            acc[b, rows] = jnp.dot(
                jnp.concatenate(ps, axis=1).astype(jnp.bfloat16), val_mat, preferred_element_type=jnp.float32
            )

    def later_unit(b, planes):
        key_mat = jnp.concatenate([kv[p, a, 0] for p in planes for a in range(2)], axis=0)
        val_mat = jnp.concatenate([kv[p, a, 1] for p in planes for a in range(2)], axis=0)
        for heads in TILES:
            rows = pl.ds(heads[0] * ROWS, (heads[1] - heads[0]) * ROWS)
            gs = scores(b, heads, key_mat)
            old = m_acc[b, rows]
            m = jnp.maximum(old, top(gs))
            alpha = jnp.exp2(old - m)
            ps = [jnp.exp2(g - m) for g in gs]
            m_acc[b, rows] = m
            l_acc[b, rows] = l_acc[b, rows] * alpha + total(ps)
            acc[b, rows] = acc[b, rows] * alpha + jnp.dot(
                jnp.concatenate(ps, axis=1).astype(jnp.bfloat16), val_mat, preferred_element_type=jnp.float32
            )

    def unit(b, s):
        ahead, behind = (z + zs - s) % zs, (z + s) % zs
        both = (z + s >= zs) & (s < fs)
        single = (z >= s) & jnp.logical_not(both) & (s > 0)

        @pl.when(s == 0)
        def _():
            first_unit(b)

        @pl.when(both)
        def _():
            later_unit(b, (ahead, behind))

        @pl.when(single)
        def _():
            later_unit(b, (ahead,))

    lane_id = lax.broadcasted_iota(jnp.int32, (ROWS, D), 1)

    def sink_pass(b):
        spot = lax.broadcasted_iota(jnp.int32, (ROWS, D), 1)
        hit = spot == sink_ref[0]
        for n in range(1, 4):
            hit = hit | (spot == sink_ref[n])
        row = lax.broadcasted_iota(jnp.int32, (ROWS, D), 0) + base * ROWS + owner(b) * ROWS
        hit = hit & (spot <= row)
        out = jnp.zeros((ROWS, D), jnp.float32)
        key_mat = kv[0, 0, 0]
        for heads in TILES:
            (s,) = scores(b, heads, key_mat)
            for j in range(heads[1] - heads[0]):
                g = jnp.where(hit, s[j * ROWS : (j + 1) * ROWS], 2 * NEG)
                m = jnp.max(g, axis=1, keepdims=True)
                r = m + jnp.log2(jnp.sum(jnp.exp2(g - m), axis=1, keepdims=True))
                out = jnp.where(lane_id == 8 + heads[0] + j, r, out)
        statb[b] = out

    reach = jnp.where(z <= fs, z, zs - z)
    early = min(max(2 * fs - 4, Q_DIAG), 2 * fs - 1)
    sink_half = jnp.where(2 * reach - 1 <= early, early, 2 * fs - 1)

    def count(b, h):
        own = 1 + (h + 1) // 2
        late = 1 + h // 2
        begun = lambda start, cap: jnp.minimum(cap, jnp.maximum(0, 2 * (h + 1 - start)))
        last = h >= 2 * fs - 1
        n = jnp.where(
            b == OWN, jnp.where(h < 0, 0, own),
            jnp.where(b == PART, begun(Q_PART, own), jnp.where(b == HEAD, begun(Q_HEAD_1, late), begun(Q_DIAG, late))),
        )
        return jnp.where(last, fs + 1, n)

    q_head_0, q_part, q_head_1, q_diag = (min(t, 2 * fs - 1) for t in (Q_HEAD_0, Q_PART, Q_HEAD_1, Q_DIAG))

    def half_step(h, carry):
        s = 1 + h // 2
        c = (mine + h) % 2
        ahead, behind = (z + zs - s) % zs, (z + s) % zs
        arrived(0, s, c, ahead).wait_recv()

        @pl.when(s < fs)
        def _():
            hop(0, s, c, ahead).start()

            arrived(1, s, c, behind).wait_recv()

        @pl.when(s < fs - 1)
        def _():
            hop(1, s, c, behind).start()

        @pl.when(h == q_head_0)
        def _():
            q_copy(0).wait_recv()
            q_copy(3).start()

        @pl.when(h == q_part)
        def _():
            q_copy(2).wait_recv()

        @pl.when(h == q_head_1)
        def _():
            q_copy(1).wait_recv()
            q_copy(4).start()

        @pl.when(h == q_diag)
        def _():
            q_copy(3).wait_recv()
            q_copy(4).wait_recv()

        def block(i, carry):
            b = 3 - i
            lo = jnp.where(h == 0, 0, count(b, h - 1))

            def one(u, carry):
                unit(b, u)
                return carry

            return lax.fori_loop(lo, count(b, h), one, carry)

        lax.fori_loop(0, 4, block, 0)

        @pl.when((h == sink_half) & (part == 0))
        def _():
            def one(b, carry):
                sink_pass(b)
                return carry

            lax.fori_loop(0, 4, one, 0)

        return carry

    @pl.when(part != 0)
    def _():
        statb[...] = jnp.zeros_like(statb)

    lax.fori_loop(0, 2 * fs, half_step, 0)

    def norm(b, carry):
        out = statb[b]
        for j in range(GROUP):
            rows = pl.ds(j * ROWS, ROWS)
            l = jnp.sum(l_acc[b, rows], axis=1, keepdims=True)
            r = jnp.where(l > 0, m_acc[b, rows] + jnp.log2(l), NEG)
            out = jnp.where(lane_id == j, r, out)
            l_acc[b, rows] = jnp.broadcast_to(jnp.where(l > 0, 1.0 / l, 0.0), (ROWS, D))
        out = jnp.where((lane_id % 8 == 7) | (lane_id >= 16), 0.0, out)
        stats[y, owner(b)] = out.T[:16]
        return carry

    lax.fori_loop(0, 4, norm, 0)

    def stat_copy(k, sender):
        target = (y_head, y_part, y_diag)[k]
        return remote(stats.at[sender], stats.at[sender], st_send.at[k], st_recv.at[k], at(z, target))

    def out_block(b, i):
        for j in range(GROUP):
            rows = pl.ds(j * ROWS, ROWS)
            obuf[i, :, j * D : (j + 1) * D] = (acc[b, rows] * l_acc[b, rows]).astype(jnp.bfloat16)

    def o_copy(k):
        src, dst, target = (
            (obuf.at[0], rx.at[0], y_part),
            (obuf.at[1], rx.at[1], y_part),
            (fin, fin_rx, y_head),
        )[k]
        return remote(src, dst, o_send.at[k], o_recv.at[k], at(z, target))

    out_block(DIAG, 0)
    for k in (1, 0, 2):
        stat_copy(k, y).start()
    out_block(PART, 1)
    o_copy(0).start()
    for k, sender in enumerate((y_head, y_part, y_diag)):
        stat_copy(k, sender).wait_recv()
    o_copy(1).start()

    length = len_ref[0]
    sums = [jnp.zeros((8, D), jnp.float32) for _ in range(4)]
    for blk in range(YS):
        pos = lax.broadcasted_iota(jnp.int32, (8, D), 1) + (base + blk) * ROWS
        live = pos < length
        for g, (a, b) in enumerate(((0, 3), (1, 2))):
            x0, x1 = stats[a, blk, 0:8], stats[b, blk, 0:8]
            m = jnp.maximum(x0, x1)
            full = m + jnp.log2(jnp.exp2(x0 - m) + jnp.exp2(x1 - m))
            mass = jnp.where(live, jnp.exp2(stats[a, blk, 8:16] - full), 0.0)
            nat = jnp.where(live, full * LN2, 0.0)
            sums[g] = sums[g] + nat
            sums[2 + g] = sums[2 + g] + mass

            @pl.when(y == blk)
            def _():
                lse_ref[g * GROUP : (g + 1) * GROUP, :] = nat[:GROUP]
                mass_ref[g * GROUP : (g + 1) * GROUP, :] = mass[:GROUP]

    lane8 = lax.broadcasted_iota(jnp.int32, (8, D), 1)
    sub8 = lax.broadcasted_iota(jnp.int32, (8, D), 0)
    line = jnp.zeros((8, D), jnp.float32)
    for i, block_sum in enumerate(sums):
        col = jnp.where(sub8 < GROUP, jnp.sum(block_sum, axis=1, keepdims=True), 0.0)
        line = line + jnp.where(lane8 == sub8 + GROUP * i, col, 0.0)
    red[z] = jnp.sum(line, axis=0, keepdims=True)

    def weights(own):
        pos = lax.broadcasted_iota(jnp.int32, (8, D), 1) + (base + own) * ROWS
        live = pos < length
        x0 = stats[y, own, 0:8]
        x1 = stats[y_part, own, 0:8]
        m = jnp.maximum(x0, x1)
        full = m + jnp.log2(jnp.exp2(x0 - m) + jnp.exp2(x1 - m))
        return [jnp.where(live, jnp.exp2(x - full), 0.0) for x in (x0, x1)]

    pad = jnp.zeros((D - 32, D), jnp.float32)
    wts[...] = jnp.concatenate([*weights(y), *weights(y_head), pad], axis=0).T

    def red_copy(k):
        return remote(red.at[z], red.at[z], red_send.at[k], red_recv.at[z], at((z + k) % zs, y))

    def red_start(k, carry):
        red_copy(k).start()
        return carry

    lax.fori_loop(1, zs, red_start, 0)

    def merged(b, i, j, w):
        rows = pl.ds(j * ROWS, ROWS)
        mine_o = acc[b, rows] * (l_acc[b, rows] * wts[:, w + j : w + j + 1])
        their_o = rx[i, :, j * D : (j + 1) * D].astype(jnp.float32) * wts[:, w + 8 + j : w + 9 + j]
        return (mine_o + their_o).astype(jnp.bfloat16)

    o_copy(0).wait_recv()
    for j in range(GROUP):
        fin[:, j * D : (j + 1) * D] = merged(HEAD, 0, j, 16)
    o_copy(2).start()
    o_copy(1).wait_recv()
    for j in range(GROUP):
        tile = merged(OWN, 1, j, 0)
        obuf[2, :, j * D : (j + 1) * D] = tile
    o_copy(2).wait_recv()
    att_ref[:, :HALF] = jnp.where(first, obuf[2], fin_rx[...])
    att_ref[:, HALF:] = jnp.where(first, fin_rx[...], obuf[2])

    def red_wait(k, carry):
        src = (z + k) % zs
        remote(red.at[src], red.at[src], red_send.at[k], red_recv.at[src], at(src, y)).wait_recv()
        return carry

    lax.fori_loop(1, zs, red_wait, 0)
    result = red[0]
    for i in range(1, zs):
        result = result + red[i]
    tot_ref[...] = result / length.astype(jnp.float32)

    to_head.wait_send()
    for k in range(5):
        q_copy(k).wait_send()
    for k in range(3):
        stat_copy(k, y).wait_send()
        o_copy(k).wait_send()

    def drain(k, carry):
        red_copy(k).wait_send()
        return carry

    lax.fori_loop(1, zs, drain, 0)

    def ring_drain(s, carry):
        for c in range(2):
            hop(0, s, c, (z + zs - s) % zs).wait_send()

            @pl.when(s < fs - 1)
            def _():
                hop(1, s, c, (z + s) % zs).wait_send()

        return carry

    lax.fori_loop(0, fs, ring_drain, 0)


def body(queries, keys, values, doc_length, sink_pos, zs):
    vmem = pl.BlockSpec(memory_space=pltpu.VMEM)
    smem = pl.BlockSpec(memory_space=pltpu.SMEM)
    fs = zs // 2
    bf16, f32 = jnp.bfloat16, jnp.float32
    dma = pltpu.SemaphoreType.DMA
    attended, row_lse, sink_mass, totals = pl.pallas_call(
        functools.partial(kernel, zs),
        out_shape=(
            jax.ShapeDtypeStruct((ROWS, 2 * HALF), bf16),
            jax.ShapeDtypeStruct((2 * GROUP, ROWS), f32),
            jax.ShapeDtypeStruct((2 * GROUP, ROWS), f32),
            jax.ShapeDtypeStruct((1, D), f32),
        ),
        in_specs=[vmem, vmem, vmem, smem, smem],
        out_specs=(vmem, vmem, vmem, vmem),
        scratch_shapes=[
            pltpu.VMEM((zs, 2, 2, ROWS, D), bf16),
            pltpu.VMEM((2, ROWS, D), bf16),
            pltpu.VMEM((4, ROWS, HALF), bf16),
            pltpu.VMEM((ROWS, HALF), bf16),
            pltpu.VMEM((4, FLAT, D), f32),
            pltpu.VMEM((4, FLAT, D), f32),
            pltpu.VMEM((4, FLAT, D), f32),
            pltpu.VMEM((3, ROWS, HALF), bf16),
            pltpu.VMEM((2, ROWS, HALF), bf16),
            pltpu.VMEM((ROWS, HALF), bf16),
            pltpu.VMEM((ROWS, HALF), bf16),
            pltpu.VMEM((4, ROWS, D), f32),
            pltpu.VMEM((YS, YS, 16, ROWS), f32),
            pltpu.VMEM((zs, 1, D), f32),
            pltpu.VMEM((ROWS, D), f32),
            dma((2, fs, 2)),
            dma((2, fs + 1, 2)),
            dma,
            dma,
            dma((5,)),
            dma((5,)),
            dma((3,)),
            dma((3,)),
            dma((3,)),
            dma((3,)),
            dma((zs,)),
            dma((zs,)),
        ],
        compiler_params=pltpu.CompilerParams(
            collective_id=0, has_side_effects=True, vmem_limit_bytes=56 * 1024 * 1024
        ),
    )(queries, keys, values, doc_length, sink_pos)
    heads = 2 * GROUP
    return (attended, row_lse, sink_mass, totals[0, :heads], totals[0, heads : 2 * heads])


def solution(mesh):
    placed = (
        P(("doc", "seq"), None),
        P(("doc", "seq"), None),
        P(("doc", "seq"), None),
        P("doc"),
        P("doc"),
    )
    return jax.shard_map(
        functools.partial(body, zs=mesh.shape["seq"] // YS),
        mesh=mesh,
        in_specs=placed,
        out_specs=(
            P(("doc", "seq"), None),
            P(None, ("doc", "seq")),
            P(None, ("doc", "seq")),
            P("doc"),
            P("doc"),
        ),
        check_vma=False,
    )
```

profile of v0, /device:TPU:28, one launch (start us, length us, event | category | flops | bytes accessed | tf_op | source)
XLA Modules:
  0.0 83.3 jit_solution(2603293886058302514)
XLA Ops:
  1.3 77.7 %shard_map.92 = (bf16[128,1792]{1,0:T(8,128)(2,1)}, f32[14,128]{1,0:T(8,128)}, f32[14,128]{1,0:T(8,128)}, f32[1,128]{1,0:T(1,128)}) custom-call(bf16[128,1792]{1,0:T(8,128)(2,1)} %q_ref.1, bf16[128,256]{1,0:T(8,128)(2,1)} %k_ref.1, bf16[128,256]{1,0:T(8,128)(2,1)} %v_ref.1, s32[1]{0:T(128)S(6)} %copy.13.len_ref, s32[4]{0:T(128)} %sink_ref.1), custom_call_target="tpu_custom_call" | custom-call | tf_op jit(solution)/shard_map/pallas_call | solution.py:427
  79.0 0.0 copy-start.2
  79.0 0.6 copy-done.2
  79.6 0.6 slice_bitcast_fusion
  80.2 0.0 copy-start.1
  80.2 1.8 %copy.14 = bf16[128,1792]{1,0:T(8,128)(2,1)} copy(bf16[128,1792]{1,0:T(8,128)(2,1)} %get-tuple-element.20) | data formatting | bytes 917504
  82.0 0.0 copy-done.1
  82.0 0.0 copy-start
  82.0 0.6 copy.15
  82.6 0.1 copy-done
  82.7 0.6 copy.16
Async XLA Ops:
  79.0 0.6 copy-start.2
  80.2 1.8 %copy-start.1 = (f32[14,128]{1,0:T(8,128)S(1)}, f32[14,128]{1,0:T(8,128)}, u32[]{:S(2)}) copy-start(f32[14,128]{1,0:T(8,128)} %get-tuple-element.21) | copy-start | bytes 21508
  82.0 0.7 copy-start
where the time goes:
time: 83.6 us; the launch traced here: 83.3 us
  Pallas kernels  77.7 us (93%)
  local copies, waits for them, and re-layouts  4.34 us (5%)
  between operations  1.3 us (2%)
    pallas_call x1, Pallas kernels, body(): pl.pallas_call(functools.partial(kernel, zs), out_shape=(jax.ShapeDtypeSt...  77.7 us
    unnamed x9, local copies, waits for them, and re-layouts  3.76 us

commit v1 on v0

--- a/solution.py
+++ b/solution.py
@@ -18,17 +18,18 @@
 SCALE = LOG2E * D**-0.5
 NEG = -1e30
 MESH = pl.DeviceIdType.MESH
-TILES = ((0, 2), (2, 4), (4, 7))
+TILES = ((0, 7),)
+PARTS = ((0, 2), (2, 4), (4, 6), (6, 7))
 OWN, PART, HEAD, DIAG = range(4)
-Q_HEAD_0, Q_PART, Q_HEAD_1, Q_DIAG = 2, 3, 4, 8
+Q_HEAD_0, Q_PART, Q_HEAD_1, Q_DIAG = 1, 2, 3, 5
 
 
 def kernel(
-    zs, q_ref, k_ref, v_ref, len_ref, sink_ref,
-    att_ref, lse_ref, mass_ref, tot_ref,
+    zs, q_ref, kv_ref, len_ref, sink_ref,
+    att_ref, small_ref,
     kv, xbuf, qbuf, qsend, acc, l_acc, m_acc, obuf, rx, fin, fin_rx, statb, stats, red, wts,
     ring_send, ring_recv, x_send, x_recv, q_send, q_recv, st_send, st_recv, o_send, o_recv,
-    red_send, red_recv,
+    red_send, red_recv, in_sem,
 ):
     fs = zs // 2
     seq = lax.axis_index("seq")
@@ -51,31 +52,36 @@
 
     first = head == 0
     mine = y % 2
-    for i, ref in enumerate((k_ref, v_ref)):
-        lo, hi = ref[:, :D], ref[:, D:]
+    wide = pl.multiple_of(head * HALF, D)
+    wide_x = pl.multiple_of((1 - head) * HALF, D)
+    into_place = [
+        pltpu.make_async_copy(q_ref.at[:, pl.ds(wide_x, HALF)], qsend, in_sem.at[0]),
+        pltpu.make_async_copy(q_ref.at[:, pl.ds(wide, HALF)], qbuf.at[OWN], in_sem.at[1]),
+    ]
+    for copy in into_place:
+        copy.start()
+    for i in range(2):
+        lo, hi = kv_ref[:, 2 * i * D : (2 * i + 1) * D], kv_ref[:, (2 * i + 1) * D : (2 * i + 2) * D]
         kv[z, mine, i] = jnp.where(first, lo, hi)
         xbuf[i] = jnp.where(first, hi, lo)
-    qlo, qhi = q_ref[:, :HALF], q_ref[:, HALF:]
-    qbuf[OWN] = jnp.where(first, qlo, qhi)
-    qsend[...] = jnp.where(first, qhi, qlo)
 
     barrier = pltpu.get_barrier_semaphore()
     for target in (at(right, y), at(left, y), at(z, y_head), at(z, y_part), at(z, y_diag)):
         pl.semaphore_signal(barrier, inc=1, device_id=target, device_id_type=MESH)
     pl.semaphore_wait(barrier, 5)
 
-    def hop(direction, s, c, plane):
+    def hop(direction, s, c, plane, i):
         return remote(
-            kv.at[plane, c], kv.at[plane, c],
-            ring_send.at[direction, s, c], ring_recv.at[direction, s + 1, c],
-            at(right if direction == 0 else left, y),
+            kv.at[plane, c, i], kv.at[plane, c, i],
+            ring_send.at[direction, s, 2 * c + i], ring_recv.at[direction, s + 1, 2 * c + i],
+            at(left if direction == 0 else right, y),
         )
 
-    def arrived(direction, s, c, plane):
+    def arrived(direction, s, c, plane, i):
         return remote(
-            kv.at[plane, c], kv.at[plane, c],
-            ring_send.at[direction, s - 1, c], ring_recv.at[direction, s, c],
-            at(right if direction == 0 else left, y),
+            kv.at[plane, c, i], kv.at[plane, c, i],
+            ring_send.at[direction, s - 1, 2 * c + i], ring_recv.at[direction, s, 2 * c + i],
+            at(left if direction == 0 else right, y),
         )
 
     def q_copy(k):
@@ -93,14 +99,18 @@
     to_head = remote(xbuf, kv.at[z, mine], x_send, x_recv, at(z, y_head))
     from_head = remote(xbuf, kv.at[z, other], x_send, x_recv, at(z, y_head))
     to_head.start()
-    hop(0, 0, mine, z).start()
-    hop(1, 0, mine, z).start()
+    for i in range(2):
+        hop(0, 0, mine, z, i).start()
+        hop(1, 0, mine, z, i).start()
+    for copy in into_place:
+        copy.wait()
     q_copy(0).start()
     q_copy(1).start()
     q_copy(2).start()
     from_head.wait_recv()
-    hop(0, 0, other, z).start()
-    hop(1, 0, other, z).start()
+    for i in range(2):
+        hop(0, 0, other, z, i).start()
+        hop(1, 0, other, z, i).start()
 
     def owner(b):
         return jnp.where(b == OWN, y, jnp.where(b == PART, y_part, jnp.where(b == HEAD, y_head, y_diag)))
@@ -159,9 +169,10 @@
             )
 
     def unit(b, s):
-        ahead, behind = (z + zs - s) % zs, (z + s) % zs
-        both = (z + s >= zs) & (s < fs)
-        single = (z >= s) & jnp.logical_not(both) & (s > 0)
+        below, above = (z + zs - s) % zs, (z + s) % zs
+        up = (s > 0) & (s < fs) & (z >= s)
+        down = (s > 0) & (z + s >= zs)
+        both = up & down
 
         @pl.when(s == 0)
         def _():
@@ -169,11 +180,11 @@
 
         @pl.when(both)
         def _():
-            later_unit(b, (ahead, behind))
-
-        @pl.when(single)
-        def _():
-            later_unit(b, (ahead,))
+            later_unit(b, (below, above))
+
+        @pl.when(up != down)
+        def _():
+            later_unit(b, (jnp.where(up, below, above),))
 
     lane_id = lax.broadcasted_iota(jnp.int32, (ROWS, D), 1)
 
@@ -195,7 +206,7 @@
                 out = jnp.where(lane_id == 8 + heads[0] + j, r, out)
         statb[b] = out
 
-    reach = jnp.where(z <= fs, z, zs - z)
+    reach = jnp.where(z < fs, z, zs - z)
     early = min(max(2 * fs - 4, Q_DIAG), 2 * fs - 1)
     sink_half = jnp.where(2 * reach - 1 <= early, early, 2 * fs - 1)
 
@@ -215,18 +226,19 @@
     def half_step(h, carry):
         s = 1 + h // 2
         c = (mine + h) % 2
-        ahead, behind = (z + zs - s) % zs, (z + s) % zs
-        arrived(0, s, c, ahead).wait_recv()
-
-        @pl.when(s < fs)
-        def _():
-            hop(0, s, c, ahead).start()
-
-            arrived(1, s, c, behind).wait_recv()
-
-        @pl.when(s < fs - 1)
-        def _():
-            hop(1, s, c, behind).start()
+        ahead, behind = (z + s) % zs, (z + zs - s) % zs
+        for i in range(2):
+            arrived(0, s, c, ahead, i).wait_recv()
+
+            @pl.when(s < fs)
+            def _():
+                hop(0, s, c, ahead, i).start()
+
+                arrived(1, s, c, behind, i).wait_recv()
+
+            @pl.when(s < fs - 1)
+            def _():
+                hop(1, s, c, behind, i).start()
 
         @pl.when(h == q_head_0)
         def _():
@@ -298,22 +310,26 @@
             rows = pl.ds(j * ROWS, ROWS)
             obuf[i, :, j * D : (j + 1) * D] = (acc[b, rows] * l_acc[b, rows]).astype(jnp.bfloat16)
 
-    def o_copy(k):
+    def o_copy(k, n):
+        lanes = slice(PARTS[n][0] * D, PARTS[n][1] * D)
         src, dst, target = (
-            (obuf.at[0], rx.at[0], y_part),
-            (obuf.at[1], rx.at[1], y_part),
-            (fin, fin_rx, y_head),
+            (obuf.at[0, :, lanes], rx.at[0, :, lanes], y_part),
+            (obuf.at[1, :, lanes], rx.at[1, :, lanes], y_part),
+            (fin.at[:, lanes], fin_rx.at[:, lanes], y_head),
         )[k]
-        return remote(src, dst, o_send.at[k], o_recv.at[k], at(z, target))
-
+        return remote(src, dst, o_send.at[k, n], o_recv.at[k, n], at(z, target))
+
+    pieces = range(len(PARTS))
     out_block(DIAG, 0)
     for k in (1, 0, 2):
         stat_copy(k, y).start()
     out_block(PART, 1)
-    o_copy(0).start()
+    for n in pieces:
+        o_copy(0, n).start()
+    for n in pieces:
+        o_copy(1, n).start()
     for k, sender in enumerate((y_head, y_part, y_diag)):
         stat_copy(k, sender).wait_recv()
-    o_copy(1).start()
 
     length = len_ref[0]
     sums = [jnp.zeros((8, D), jnp.float32) for _ in range(4)]
@@ -331,8 +347,8 @@
 
             @pl.when(y == blk)
             def _():
-                lse_ref[g * GROUP : (g + 1) * GROUP, :] = nat[:GROUP]
-                mass_ref[g * GROUP : (g + 1) * GROUP, :] = mass[:GROUP]
+                small_ref[g * GROUP : (g + 1) * GROUP, :] = nat[:GROUP]
+                small_ref[16 + g * GROUP : 16 + (g + 1) * GROUP, :] = mass[:GROUP]
 
     lane8 = lax.broadcasted_iota(jnp.int32, (8, D), 1)
     sub8 = lax.broadcasted_iota(jnp.int32, (8, D), 0)
@@ -369,15 +385,17 @@
         their_o = rx[i, :, j * D : (j + 1) * D].astype(jnp.float32) * wts[:, w + 8 + j : w + 9 + j]
         return (mine_o + their_o).astype(jnp.bfloat16)
 
-    o_copy(0).wait_recv()
-    for j in range(GROUP):
-        fin[:, j * D : (j + 1) * D] = merged(HEAD, 0, j, 16)
-    o_copy(2).start()
-    o_copy(1).wait_recv()
-    for j in range(GROUP):
-        tile = merged(OWN, 1, j, 0)
-        obuf[2, :, j * D : (j + 1) * D] = tile
-    o_copy(2).wait_recv()
+    for n in pieces:
+        o_copy(0, n).wait_recv()
+        for j in range(*PARTS[n]):
+            fin[:, j * D : (j + 1) * D] = merged(HEAD, 0, j, 16)
+        o_copy(2, n).start()
+    for n in pieces:
+        o_copy(1, n).wait_recv()
+        for j in range(*PARTS[n]):
+            obuf[2, :, j * D : (j + 1) * D] = merged(OWN, 1, j, 0)
+    for n in pieces:
+        o_copy(2, n).wait_recv()
     att_ref[:, :HALF] = jnp.where(first, obuf[2], fin_rx[...])
     att_ref[:, HALF:] = jnp.where(first, fin_rx[...], obuf[2])
 
@@ -390,14 +408,17 @@
     result = red[0]
     for i in range(1, zs):
         result = result + red[i]
-    tot_ref[...] = result / length.astype(jnp.float32)
+    result = result / length.astype(jnp.float32)
+    small_ref[30:31, : 2 * GROUP] = result[:, : 2 * GROUP]
+    small_ref[31:32, : 2 * GROUP] = result[:, 2 * GROUP : 4 * GROUP]
 
     to_head.wait_send()
     for k in range(5):
         q_copy(k).wait_send()
     for k in range(3):
         stat_copy(k, y).wait_send()
-        o_copy(k).wait_send()
+        for n in pieces:
+            o_copy(k, n).wait_send()
 
     def drain(k, carry):
         red_copy(k).wait_send()
@@ -407,33 +428,41 @@
 
     def ring_drain(s, carry):
         for c in range(2):
-            hop(0, s, c, (z + zs - s) % zs).wait_send()
-
-            @pl.when(s < fs - 1)
-            def _():
-                hop(1, s, c, (z + s) % zs).wait_send()
+            for i in range(2):
+                hop(0, s, c, (z + s) % zs, i).wait_send()
+
+                @pl.when(s < fs - 1)
+                def _():
+                    hop(1, s, c, (z + zs - s) % zs, i).wait_send()
 
         return carry
 
     lax.fori_loop(0, fs, ring_drain, 0)
+
+
+def spread(att_in, small_ref, att_ref, lse_ref, mass_ref, head_lse_ref, head_sink_ref):
+    att_ref[...] = att_in[...]
+    lse_ref[...] = small_ref[: 2 * GROUP]
+    mass_ref[...] = small_ref[16 : 16 + 2 * GROUP]
+    head_lse_ref[...] = small_ref[30:31, : 2 * GROUP]
+    head_sink_ref[...] = small_ref[31:32, : 2 * GROUP]
 
 
 def body(queries, keys, values, doc_length, sink_pos, zs):
     vmem = pl.BlockSpec(memory_space=pltpu.VMEM)
     smem = pl.BlockSpec(memory_space=pltpu.SMEM)
+    hbm = pl.BlockSpec(memory_space=pltpu.HBM)
     fs = zs // 2
     bf16, f32 = jnp.bfloat16, jnp.float32
     dma = pltpu.SemaphoreType.DMA
-    attended, row_lse, sink_mass, totals = pl.pallas_call(
+    attended, small = pl.pallas_call(
         functools.partial(kernel, zs),
         out_shape=(
             jax.ShapeDtypeStruct((ROWS, 2 * HALF), bf16),
-            jax.ShapeDtypeStruct((2 * GROUP, ROWS), f32),
-            jax.ShapeDtypeStruct((2 * GROUP, ROWS), f32),
-            jax.ShapeDtypeStruct((1, D), f32),
+            jax.ShapeDtypeStruct((32, ROWS), f32),
         ),
-        in_specs=[vmem, vmem, vmem, smem, smem],
-        out_specs=(vmem, vmem, vmem, vmem),
+        in_specs=[hbm, vmem, smem, smem],
+        out_specs=(vmem, vmem),
         scratch_shapes=[
             pltpu.VMEM((zs, 2, 2, ROWS, D), bf16),
             pltpu.VMEM((2, ROWS, D), bf16),
@@ -450,25 +479,39 @@
             pltpu.VMEM((YS, YS, 16, ROWS), f32),
             pltpu.VMEM((zs, 1, D), f32),
             pltpu.VMEM((ROWS, D), f32),
-            dma((2, fs, 2)),
-            dma((2, fs + 1, 2)),
+            dma((2, fs, 4)),
+            dma((2, fs + 1, 4)),
             dma,
             dma,
             dma((5,)),
             dma((5,)),
             dma((3,)),
             dma((3,)),
-            dma((3,)),
-            dma((3,)),
+            dma((3, len(PARTS))),
+            dma((3, len(PARTS))),
             dma((zs,)),
             dma((zs,)),
+            dma((2,)),
         ],
         compiler_params=pltpu.CompilerParams(
-            collective_id=0, has_side_effects=True, vmem_limit_bytes=56 * 1024 * 1024
+            collective_id=0, has_side_effects=True, vmem_limit_bytes=53 * 1024 * 1024 + 192 * 1024
         ),
-    )(queries, keys, values, doc_length, sink_pos)
+    )(queries, jnp.concatenate([keys, values], axis=1), doc_length, sink_pos)
     heads = 2 * GROUP
-    return (attended, row_lse, sink_mass, totals[0, :heads], totals[0, heads : 2 * heads])
+    attended, row_lse, sink_mass, head_lse, head_sink = pl.pallas_call(
+        spread,
+        out_shape=(
+            jax.ShapeDtypeStruct((ROWS, 2 * HALF), bf16),
+            jax.ShapeDtypeStruct((heads, ROWS), f32),
+            jax.ShapeDtypeStruct((heads, ROWS), f32),
+            jax.ShapeDtypeStruct((1, heads), f32),
+            jax.ShapeDtypeStruct((1, heads), f32),
+        ),
+        in_specs=[vmem, vmem],
+        out_specs=(vmem,) * 5,
+        compiler_params=pltpu.CompilerParams(vmem_limit_bytes=4 * 1024 * 1024),
+    )(attended, small)
+    return (attended, row_lse, sink_mass, head_lse[0], head_sink[0])
 
 
 def solution(mesh):

time: 83.6 us -> 70.4 us (0.84)
  the two profiles are of different devices: /device:TPU:28 before, /device:TPU:26 now
where the time goes in v1:
time: 70.4 us; the launch traced here: 70.2 us
  Pallas kernels  68 us (97%)
  between operations  1.31 us (2%)
  other arithmetic  0.89 us (1%)
    pallas_call x1, Pallas kernels, body(): pl.pallas_call(functools.partial(kernel, zs), out_shape=(jax.ShapeDtypeSt...  67.2 us

profile of v1, /device:TPU:26, one launch (start us, length us, event | category | flops | bytes accessed | tf_op | source)
XLA Modules:
  0.0 70.2 jit_solution(18204439082928602779)
XLA Ops:
  1.3 0.0 copy-start
  1.3 0.9 %pad_maximum_fusion.kv_ref = bf16[128,512]{1,0:T(8,128)(2,1)S(1)} fusion(bf16[128,256]{1,0:T(8,128)(2,1)} %param.7, bf16[128,256]{1,0:T(8,128)(2,1)} %param.6), kind=kLoop, calls=%fused_computation | loop fusion | flops 262144 | bytes 262144 | tf_op jit(solution)/shard_map/concatenate | solution.py:499
  2.2 0.0 copy-done
  2.2 67.2 %shard_map.92 = (bf16[128,1792]{1,0:T(8,128)(2,1)S(1)}, f32[32,128]{1,0:T(8,128)S(1)}) custom-call(bf16[128,1792]{1,0:T(8,128)(2,1)} %q_ref.1, bf16[128,512]{1,0:T(8,128)(2,1)S(1)} %pad_maximum_fusion.kv_ref, s32[1]{0:T(128)S(6)} %copy.10.len_ref, s32[4]{0:T(128)S(1)} %copy-done), custom_call_target="tpu_custom_call" | custom-call | tf_op jit(solution)/shard_map/pallas_call | solution.py:458
  69.4 0.8 %shard_map.93 = (bf16[128,1792]{1,0:T(8,128)(2,1)}, f32[14,128]{1,0:T(8,128)}, f32[14,128]{1,0:T(8,128)}, f32[1,14]{1,0:T(1,128)}, f32[1,14]{1,0:T(1,128)}) custom-call(bf16[128,1792]{1,0:T(8,128)(2,1)S(1)} %get-tuple-element.12.att_in, f32[32,128]{1,0:T(8,128)S(1)} %get-tuple-element.13.small_ref), custom_call_target="tpu_custom_call" | custom-call | tf_op jit(solution)/shard_map/pallas_call | solution.py:501
Async XLA Ops:
  1.3 0.9 %copy-start = (s32[4]{0:T(128)S(1)}, s32[4]{0:T(128)}, u32[]{:S(2)}) copy-start(s32[4]{0:T(128)} %sink_ref.1) | copy-start | bytes 52

commit v2 on v1

--- a/solution.py
+++ b/solution.py
@@ -21,13 +21,13 @@
 TILES = ((0, 7),)
 PARTS = ((0, 2), (2, 4), (4, 6), (6, 7))
 OWN, PART, HEAD, DIAG = range(4)
-Q_HEAD_0, Q_PART, Q_HEAD_1, Q_DIAG = 1, 2, 3, 5
+Q_HEAD_0, Q_PART, Q_HEAD_1, Q_DIAG = 3, 5, 7, 11
 
 
 def kernel(
     zs, q_ref, kv_ref, len_ref, sink_ref,
     att_ref, small_ref,
-    kv, xbuf, qbuf, qsend, acc, l_acc, m_acc, obuf, rx, fin, fin_rx, statb, stats, red, wts,
+    kv, xbuf, qbuf, qsend, acc, l_acc, m_acc, obuf, rx, fin, fin_rx, stats, red, wts,
     ring_send, ring_recv, x_send, x_recv, q_send, q_recv, st_send, st_recv, o_send, o_recv,
     red_send, red_recv, in_sem,
 ):
@@ -119,7 +119,7 @@
         lo, hi = heads
         rows = jnp.concatenate([qbuf[b, :, j * D : (j + 1) * D] for j in range(lo, hi)], axis=0)
         s = lax.dot_general(rows, key_mat, (((1,), (1,)), ((), ())), preferred_element_type=jnp.float32)
-        return [s[:, j : j + D] * SCALE for j in range(0, key_mat.shape[0], D)]
+        return [s[:, j : j + D] for j in range(0, key_mat.shape[0], D)]
 
     def top(groups):
         best = groups[0]
@@ -143,7 +143,7 @@
             row = lax.broadcasted_iota(jnp.int32, (n, D), 0) % ROWS + owner(b) * ROWS
             lane = lax.broadcasted_iota(jnp.int32, (n, D), 1) + part * (2 * ROWS)
             ok = [lane + j * D <= row for j in range(2)]
-            gs = [jnp.where(o, g, 2 * NEG) for o, g in zip(ok, gs)]
+            gs = [jnp.where(o, g * SCALE, 2 * NEG) for o, g in zip(ok, gs)]
             m = jnp.maximum(top(gs), NEG)
             ps = [jnp.exp2(g - m) for g in gs]
             m_acc[b, rows] = m
@@ -159,9 +159,9 @@
             rows = pl.ds(heads[0] * ROWS, (heads[1] - heads[0]) * ROWS)
             gs = scores(b, heads, key_mat)
             old = m_acc[b, rows]
-            m = jnp.maximum(old, top(gs))
+            m = jnp.maximum(old, top(gs) * SCALE)
             alpha = jnp.exp2(old - m)
-            ps = [jnp.exp2(g - m) for g in gs]
+            ps = [jnp.exp2(g * SCALE - m) for g in gs]
             m_acc[b, rows] = m
             l_acc[b, rows] = l_acc[b, rows] * alpha + total(ps)
             acc[b, rows] = acc[b, rows] * alpha + jnp.dot(
@@ -188,115 +188,110 @@
 
     lane_id = lax.broadcasted_iota(jnp.int32, (ROWS, D), 1)
 
-    def sink_pass(b):
-        spot = lax.broadcasted_iota(jnp.int32, (ROWS, D), 1)
-        hit = spot == sink_ref[0]
-        for n in range(1, 4):
-            hit = hit | (spot == sink_ref[n])
-        row = lax.broadcasted_iota(jnp.int32, (ROWS, D), 0) + base * ROWS + owner(b) * ROWS
-        hit = hit & (spot <= row)
-        out = jnp.zeros((ROWS, D), jnp.float32)
-        key_mat = kv[0, 0, 0]
-        for heads in TILES:
-            (s,) = scores(b, heads, key_mat)
-            for j in range(heads[1] - heads[0]):
-                g = jnp.where(hit, s[j * ROWS : (j + 1) * ROWS], 2 * NEG)
-                m = jnp.max(g, axis=1, keepdims=True)
-                r = m + jnp.log2(jnp.sum(jnp.exp2(g - m), axis=1, keepdims=True))
-                out = jnp.where(lane_id == 8 + heads[0] + j, r, out)
-        statb[b] = out
+    def sink_keys():
+        row = lax.broadcasted_iota(jnp.int32, (16, D), 0)
+        spot = lax.broadcasted_iota(jnp.int32, (16, D), 1)
+        where = jnp.full((16, D), 1 << 20, jnp.int32)
+        for n in range(4):
+            where = jnp.where(row == n, sink_ref[n], where)
+        pick = jnp.where(spot == where, 1.0, 0.0).astype(jnp.bfloat16)
+        keys = jnp.dot(pick, kv[0, 0, 0], preferred_element_type=jnp.float32)
+        return keys.astype(jnp.bfloat16), where
+
+    def sink_pass(b, key_mat, where):
+        rows = jnp.concatenate([qbuf[b, :, j * D : (j + 1) * D] for j in range(GROUP)], axis=0)
+        s = lax.dot_general(key_mat, rows, (((1,), (1,)), ((), ())), preferred_element_type=jnp.float32)
+        pos = lax.broadcasted_iota(jnp.int32, (16, D), 1) + (base + owner(b)) * ROWS
+        for j in range(GROUP):
+            g = jnp.where(where <= pos, s[:, j * D : (j + 1) * D] * SCALE, 2 * NEG)
+            m = jnp.max(g, axis=0, keepdims=True)
+            stats[y, owner(b), 8 + j : 9 + j, :] = m + jnp.log2(jnp.sum(jnp.exp2(g - m), axis=0, keepdims=True))
 
     reach = jnp.where(z < fs, z, zs - z)
-    early = min(max(2 * fs - 4, Q_DIAG), 2 * fs - 1)
-    sink_half = jnp.where(2 * reach - 1 <= early, early, 2 * fs - 1)
-
-    def count(b, h):
-        own = 1 + (h + 1) // 2
-        late = 1 + h // 2
-        begun = lambda start, cap: jnp.minimum(cap, jnp.maximum(0, 2 * (h + 1 - start)))
-        last = h >= 2 * fs - 1
-        n = jnp.where(
-            b == OWN, jnp.where(h < 0, 0, own),
-            jnp.where(b == PART, begun(Q_PART, own), jnp.where(b == HEAD, begun(Q_HEAD_1, late), begun(Q_DIAG, late))),
-        )
-        return jnp.where(last, fs + 1, n)
-
-    q_head_0, q_part, q_head_1, q_diag = (min(t, 2 * fs - 1) for t in (Q_HEAD_0, Q_PART, Q_HEAD_1, Q_DIAG))
-
-    def half_step(h, carry):
-        s = 1 + h // 2
-        c = (mine + h) % 2
+    last = 4 * fs - 1
+    early = min(max(4 * fs - 8, Q_DIAG), last)
+    sink_step = jnp.minimum(jnp.maximum(4 * reach, early), last)
+
+    def count(b, k):
+        begin = jnp.where(b == OWN, 0, jnp.where(b == PART, q_part, jnp.where(b == HEAD, q_head_1, q_diag)))
+        n = jnp.minimum(1 + jnp.maximum(k + 1 - b, 0) // 4, jnp.maximum(k + 1 - begin, 0))
+        return jnp.where(k >= last, fs + 1, n)
+
+    q_head_0, q_part, q_head_1, q_diag = (min(t, last) for t in (Q_HEAD_0, Q_PART, Q_HEAD_1, Q_DIAG))
+
+    def quarter_step(k, carry):
+        s = 1 + k // 4
+        c = (mine + (k % 4) // 2) % 2
+        i = k % 2
         ahead, behind = (z + s) % zs, (z + zs - s) % zs
-        for i in range(2):
-            arrived(0, s, c, ahead, i).wait_recv()
-
-            @pl.when(s < fs)
-            def _():
-                hop(0, s, c, ahead, i).start()
-
-                arrived(1, s, c, behind, i).wait_recv()
-
-            @pl.when(s < fs - 1)
-            def _():
-                hop(1, s, c, behind, i).start()
-
-        @pl.when(h == q_head_0)
+        arrived(0, s, c, ahead, i).wait_recv()
+
+        @pl.when(s < fs)
+        def _():
+            hop(0, s, c, ahead, i).start()
+
+            arrived(1, s, c, behind, i).wait_recv()
+
+        @pl.when(s < fs - 1)
+        def _():
+            hop(1, s, c, behind, i).start()
+
+        @pl.when(k == q_head_0)
         def _():
             q_copy(0).wait_recv()
             q_copy(3).start()
 
-        @pl.when(h == q_part)
+        @pl.when(k == q_part)
         def _():
             q_copy(2).wait_recv()
 
-        @pl.when(h == q_head_1)
+        @pl.when(k == q_head_1)
         def _():
             q_copy(1).wait_recv()
             q_copy(4).start()
 
-        @pl.when(h == q_diag)
+        @pl.when(k == q_diag)
         def _():
             q_copy(3).wait_recv()
             q_copy(4).wait_recv()
 
         def block(i, carry):
             b = 3 - i
-            lo = jnp.where(h == 0, 0, count(b, h - 1))
+            lo = jnp.where(k == 0, 0, count(b, k - 1))
 
             def one(u, carry):
                 unit(b, u)
                 return carry
 
-            return lax.fori_loop(lo, count(b, h), one, carry)
+            return lax.fori_loop(lo, count(b, k), one, carry)
 
         lax.fori_loop(0, 4, block, 0)
 
-        @pl.when((h == sink_half) & (part == 0))
-        def _():
+        @pl.when((k == sink_step) & (part == 0))
+        def _():
+            key_mat, where = sink_keys()
+
             def one(b, carry):
-                sink_pass(b)
+                sink_pass(b, key_mat, where)
                 return carry
 
             lax.fori_loop(0, 4, one, 0)
 
         return carry
 
-    @pl.when(part != 0)
-    def _():
-        statb[...] = jnp.zeros_like(statb)
-
-    lax.fori_loop(0, 2 * fs, half_step, 0)
+    stats[y] = jnp.zeros((YS, 16, ROWS), jnp.float32)
+
+    lax.fori_loop(0, 4 * fs, quarter_step, 0)
 
     def norm(b, carry):
-        out = statb[b]
+        out = jnp.zeros((ROWS, D), jnp.float32)
         for j in range(GROUP):
             rows = pl.ds(j * ROWS, ROWS)
             l = jnp.sum(l_acc[b, rows], axis=1, keepdims=True)
             r = jnp.where(l > 0, m_acc[b, rows] + jnp.log2(l), NEG)
             out = jnp.where(lane_id == j, r, out)
             l_acc[b, rows] = jnp.broadcast_to(jnp.where(l > 0, 1.0 / l, 0.0), (ROWS, D))
-        out = jnp.where((lane_id % 8 == 7) | (lane_id >= 16), 0.0, out)
-        stats[y, owner(b)] = out.T[:16]
+        stats[y, owner(b), :8, :] = out.T[:8]
         return carry
 
     lax.fori_loop(0, 4, norm, 0)
@@ -320,9 +315,9 @@
         return remote(src, dst, o_send.at[k, n], o_recv.at[k, n], at(z, target))
 
     pieces = range(len(PARTS))
+    for k in (2, 1, 0):
+        stat_copy(k, y).start()
     out_block(DIAG, 0)
-    for k in (1, 0, 2):
-        stat_copy(k, y).start()
     out_block(PART, 1)
     for n in pieces:
         o_copy(0, n).start()
@@ -373,11 +368,11 @@
     def red_copy(k):
         return remote(red.at[z], red.at[z], red_send.at[k], red_recv.at[z], at((z + k) % zs, y))
 
-    def red_start(k, carry):
-        red_copy(k).start()
+    def red_start(n, carry):
+        red_copy(fs + (2 * (n % 2) - 1) * ((n + 1) // 2)).start()
         return carry
 
-    lax.fori_loop(1, zs, red_start, 0)
+    lax.fori_loop(0, zs - 1, red_start, 0)
 
     def merged(b, i, j, w):
         rows = pl.ds(j * ROWS, ROWS)
@@ -475,7 +470,6 @@
             pltpu.VMEM((2, ROWS, HALF), bf16),
             pltpu.VMEM((ROWS, HALF), bf16),
             pltpu.VMEM((ROWS, HALF), bf16),
-            pltpu.VMEM((4, ROWS, D), f32),
             pltpu.VMEM((YS, YS, 16, ROWS), f32),
             pltpu.VMEM((zs, 1, D), f32),
             pltpu.VMEM((ROWS, D), f32),

time: 70.4 us -> 68.8 us (0.977)
  the two profiles are of different devices: /device:TPU:26 before, /device:TPU:2 now
where the time goes in v2:
time: 68.8 us; the launch traced here: 68.7 us
  Pallas kernels  66.5 us (97%)
  between operations  1.31 us (2%)
  other arithmetic  0.89 us (1%)
    pallas_call x1, Pallas kernels, body(): pl.pallas_call(functools.partial(kernel, zs), out_shape=(jax.ShapeDtypeSt...  65.7 us

profile of v2, /device:TPU:2, one launch (start us, length us, event | category | flops | bytes accessed | tf_op | source)
XLA Modules:
  0.0 68.7 jit_solution(9849956841539796634)
XLA Ops:
  1.3 0.0 copy-start
  1.3 0.9 %pad_maximum_fusion.kv_ref = bf16[128,512]{1,0:T(8,128)(2,1)S(1)} fusion(bf16[128,256]{1,0:T(8,128)(2,1)} %param.7, bf16[128,256]{1,0:T(8,128)(2,1)} %param.6), kind=kLoop, calls=%fused_computation | loop fusion | flops 262144 | bytes 262144 | tf_op jit(solution)/shard_map/concatenate | solution.py:493
  2.2 0.0 copy-done
  2.2 65.7 %shard_map.92 = (bf16[128,1792]{1,0:T(8,128)(2,1)S(1)}, f32[32,128]{1,0:T(8,128)S(1)}) custom-call(bf16[128,1792]{1,0:T(8,128)(2,1)} %q_ref.1, bf16[128,512]{1,0:T(8,128)(2,1)S(1)} %pad_maximum_fusion.kv_ref, s32[1]{0:T(128)S(6)} %copy.10.len_ref, s32[4]{0:T(128)S(1)} %copy-done), custom_call_target="tpu_custom_call" | custom-call | tf_op jit(solution)/shard_map/pallas_call | solution.py:453
  67.8 0.8 %shard_map.93 = (bf16[128,1792]{1,0:T(8,128)(2,1)}, f32[14,128]{1,0:T(8,128)}, f32[14,128]{1,0:T(8,128)}, f32[1,14]{1,0:T(1,128)}, f32[1,14]{1,0:T(1,128)}) custom-call(bf16[128,1792]{1,0:T(8,128)(2,1)S(1)} %get-tuple-element.12.att_in, f32[32,128]{1,0:T(8,128)S(1)} %get-tuple-element.13.small_ref), custom_call_target="tpu_custom_call" | custom-call | tf_op jit(solution)/shard_map/pallas_call | solution.py:495
Async XLA Ops:
  1.3 0.9 %copy-start = (s32[4]{0:T(128)S(1)}, s32[4]{0:T(128)}, u32[]{:S(2)}) copy-start(s32[4]{0:T(128)} %sink_ref.1) | copy-start | bytes 52

commit v3 on v2

--- a/solution.py
+++ b/solution.py
@@ -294,7 +294,8 @@
         stats[y, owner(b), :8, :] = out.T[:8]
         return carry
 
-    lax.fori_loop(0, 4, norm, 0)
+    for b in range(4):
+        norm(b, 0)
 
     def stat_copy(k, sender):
         target = (y_head, y_part, y_diag)[k]

time: 68.8 us -> 68.5 us (level)
  no operation moved by 1% of the time
where the time goes in v3:
time: 68.5 us; the launch traced here: 68.4 us
  Pallas kernels  66.2 us (97%)
  between operations  1.31 us (2%)
  other arithmetic  0.89 us (1%)
    pallas_call x1, Pallas kernels, body(): pl.pallas_call(functools.partial(kernel, zs), out_shape=(jax.ShapeDtypeSt...  65.4 us

profile of v3, /device:TPU:2, one launch (start us, length us, event | category | flops | bytes accessed | tf_op | source)
XLA Modules:
  0.0 68.4 jit_solution(1979556494958190914)
XLA Ops:
  1.3 0.0 copy-start
  1.3 0.9 %pad_maximum_fusion.kv_ref = bf16[128,512]{1,0:T(8,128)(2,1)S(1)} fusion(bf16[128,256]{1,0:T(8,128)(2,1)} %param.7, bf16[128,256]{1,0:T(8,128)(2,1)} %param.6), kind=kLoop, calls=%fused_computation | loop fusion | flops 262144 | bytes 262144 | tf_op jit(solution)/shard_map/concatenate | solution.py:494
  2.2 0.0 copy-done
  2.2 65.4 %shard_map.92 = (bf16[128,1792]{1,0:T(8,128)(2,1)S(1)}, f32[32,128]{1,0:T(8,128)S(1)}) custom-call(bf16[128,1792]{1,0:T(8,128)(2,1)} %q_ref.1, bf16[128,512]{1,0:T(8,128)(2,1)S(1)} %pad_maximum_fusion.kv_ref, s32[1]{0:T(128)S(6)} %copy.10.len_ref, s32[4]{0:T(128)S(1)} %copy-done), custom_call_target="tpu_custom_call" | custom-call | tf_op jit(solution)/shard_map/pallas_call | solution.py:454
  67.6 0.8 %shard_map.93 = (bf16[128,1792]{1,0:T(8,128)(2,1)}, f32[14,128]{1,0:T(8,128)}, f32[14,128]{1,0:T(8,128)}, f32[1,14]{1,0:T(1,128)}, f32[1,14]{1,0:T(1,128)}) custom-call(bf16[128,1792]{1,0:T(8,128)(2,1)S(1)} %get-tuple-element.12.att_in, f32[32,128]{1,0:T(8,128)S(1)} %get-tuple-element.13.small_ref), custom_call_target="tpu_custom_call" | custom-call | tf_op jit(solution)/shard_map/pallas_call | solution.py:496
Async XLA Ops:
  1.3 0.9 %copy-start = (s32[4]{0:T(128)S(1)}, s32[4]{0:T(128)}, u32[]{:S(2)}) copy-start(s32[4]{0:T(128)} %sink_ref.1) | copy-start | bytes 52
